TPU v7x, 32 devices: a whole 2x2x4 slice. The times are simulated.
32 devices in a mesh: fsdp: 4 (over y, x), tp: 8 (over z, core).
Axes of the slice: x: 2, y: 2, z: 4, core: 2. Of those that a mesh axis runs over, the one named last changes fastest.
Arguments:
- tokens: bfloat16 [1024, 8192], P('fsdp', 'tp'), may hold values from -6 to 6
- out_grad: bfloat16 [1024, 8192], P('fsdp', 'tp'), may hold values from -6 to 6
- gate_weight: bfloat16 [8192, 1024], P('fsdp', 'tp'), may hold values from -0.0625 to 0.0625
- up_weight: bfloat16 [8192, 1024], P('fsdp', 'tp'), may hold values from -0.0625 to 0.0625
- down_weight: bfloat16 [1024, 8192], P('tp', 'fsdp'), may hold values from -0.1875 to 0.1875
Outputs:
- input_grad: bfloat16 [1024, 8192], P('fsdp', 'tp')
- gate_grad: float32 [8192, 1024], P('fsdp', 'tp')
- up_grad: float32 [8192, 1024], P('fsdp', 'tp')
- down_grad: float32 [1024, 8192], P('tp', 'fsdp')
All inputs are finite; a program needn't handle non-finite values.
Results may differ from a plain program's by a relative error of at most 0.0023.
Values may be sent and summed in bfloat16 or wider, within the bound.
A program may use at most 128 MiB of HBM per device.

v0:
```python
import math
import jax
import jax.numpy as jnp
from jax import lax
from jax.sharding import PartitionSpec as P


def over_all(shard, axis, dim, absorb, state):
    everything = jax.tree.map(lambda a: lax.all_gather(a, axis, axis=dim, tiled=True), shard)
    return absorb(state, everything, jnp.int32(0))


def own_rows(portion, rows, axis):
    count = rows * lax.axis_size(axis)
    return lax.psum_scatter(portion(jnp.int32(0), count), axis, scatter_dimension=0, tiled=True)


def column_term(left, right, start, count, factor):
    block = lax.dynamic_slice_in_dim(left, start, count, 1)
    product = lax.dot_general(
        block, right, (((0,), (0,)), ((), ())), preferred_element_type=jnp.float32
    )
    return product * factor


def body(tokens, out_grad, gate_weight, up_weight, down_weight):
    factor = 1.0 / math.sqrt(tokens.shape[0] * lax.axis_size("fsdp"))
    whole = lax.all_gather(tokens, "tp", axis=1, tiled=True)
    grads = lax.all_gather(out_grad, "tp", axis=1, tiled=True)
    gate_full, up_full = (
        lax.all_gather(gate_weight, "fsdp", axis=0, tiled=True),
        lax.all_gather(up_weight, "fsdp", axis=0, tiled=True),
    )
    gate = jnp.dot(whole, gate_full, preferred_element_type=jnp.float32)
    up = jnp.dot(whole, up_full, preferred_element_type=jnp.float32)

    def add_down(total, piece, start):
        columns = lax.dynamic_slice_in_dim(grads, start, piece.shape[1], 1)
        return total + lax.dot_general(
            columns, piece, (((1,), (1,)), ((), ())), preferred_element_type=jnp.float32
        )

    initial = jnp.zeros((whole.shape[0], down_weight.shape[0]), jnp.float32)
    hidden_grad = over_all(down_weight, "fsdp", 1, add_down, initial)
    squashed = jax.nn.sigmoid(gate)
    activated = gate * squashed
    slope = squashed * (1.0 + gate * (1.0 - squashed))
    hidden = (activated * up).astype(jnp.bfloat16)
    gate_delta = (hidden_grad * up * slope).astype(jnp.bfloat16)
    up_delta = (hidden_grad * activated).astype(jnp.bfloat16)
    partial_term = jnp.dot(gate_delta, gate_full.T, preferred_element_type=jnp.float32)
    partial_term = partial_term + jnp.dot(up_delta, up_full.T, preferred_element_type=jnp.float32)
    input_grad = lax.psum_scatter(partial_term, "tp", scatter_dimension=1, tiled=True).astype(
        jnp.bfloat16
    )
    rows_here = gate_weight.shape[0]

    def joint_term(start, count):
        return jnp.concatenate(
            [
                column_term(whole, gate_delta, start, count, factor),
                column_term(whole, up_delta, start, count, factor),
                column_term(grads, hidden, start, count, factor),
            ],
            axis=1,
        )

    summed = own_rows(joint_term, rows_here, "fsdp")
    width = gate_delta.shape[1]
    gate_grad = summed[:, :width]
    up_grad = summed[:, width : 2 * width]
    down_grad = summed[:, 2 * width :].T
    return (input_grad, gate_grad, up_grad, down_grad)


def solution(mesh):
    return jax.shard_map(
        body,
        mesh=mesh,
        in_specs=(
            P("fsdp", "tp"),
            P("fsdp", "tp"),
            P("fsdp", "tp"),
            P("fsdp", "tp"),
            P("tp", "fsdp"),
        ),
        out_specs=(P("fsdp", "tp"), P("fsdp", "tp"), P("fsdp", "tp"), P("tp", "fsdp")),
        check_vma=False,
    )
```

profile of v0, /device:TPU:0, one launch (start us, length us, event | category | flops | bytes accessed | tf_op | source)
XLA Modules:
  0.0 450.8 jit_solution(9459281939705098741)
XLA Ops:
  7.2 0.0 all-gather.14.cloned.1.call-start
  7.2 0.7 all-gather.14.cloned.1.call-update
  7.9 0.0 all-gather.10.cloned.1.call-start
  7.9 0.7 all-gather.10.cloned.1.call-update
  8.6 0.0 all-gather.12.cloned.1.call-start
  8.7 0.7 all-gather.12.cloned.1.call-update
  9.4 0.0 all-gather.8.cloned.1.call-start
  9.4 0.5 all-gather.8.cloned.1.call-update
  10.0 0.0 all-gather.6.cloned.1.call-start
  10.0 0.5 all-gather.6.cloned.1.call-update
  10.5 0.0 reduce-scatter.3.cloned.1.call-start
  10.6 37.2 %all-gather.14.cloned.1.call-done = bf16[8192,128]{1,0:T(8,128)(2,1)} async-done(((bf16[2048,128]{1,0:T(8,128)(2,1)}), bf16[8192,128]{1,0:T(8,128)(2,1)}) %all-gather.14.cloned.1.call-update) | async-done | bytes 2097168 | tf_op jit(solution)/shard_map/all_gather | solution.py:31
  47.8 48.5 %all-gather.10.cloned.1.call-done = bf16[256,8192]{1,0:T(8,128)(2,1)} async-done(((bf16[256,1024]{1,0:T(8,128)(2,1)}), bf16[256,8192]{1,0:T(8,128)(2,1)}) %all-gather.10.cloned.1.call-update) | async-done | bytes 4194320 | tf_op jit(solution)/shard_map/all_gather | solution.py:28
  96.3 4.1 fusion.7
  100.4 31.8 %all-gather.12.cloned.1.call-done = bf16[8192,128]{1,0:T(8,128)(2,1)} async-done(((bf16[2048,128]{1,0:T(8,128)(2,1)}), bf16[8192,128]{1,0:T(8,128)(2,1)}) %all-gather.12.cloned.1.call-update) | async-done | bytes 2097168 | tf_op jit(solution)/shard_map/all_gather | solution.py:32
  132.1 4.1 fusion.6
  136.2 0.0 copy-start.1
  136.2 32.8 %all-gather.8.cloned.1.call-done = bf16[128,8192]{1,0:T(8,128)(2,1)} async-done(((bf16[128,2048]{1,0:T(8,128)(2,1)}), bf16[128,8192]{1,0:T(8,128)(2,1)}) %all-gather.8.cloned.1.call-update) | async-done | bytes 2097168 | tf_op jit(solution)/shard_map/all_gather | solution.py:9
  169.0 48.4 %all-gather.6.cloned.1.call-done = bf16[256,8192]{1,0:T(8,128)(2,1)} async-done(((bf16[256,1024]{1,0:T(8,128)(2,1)}), bf16[256,8192]{1,0:T(8,128)(2,1)}) %all-gather.6.cloned.1.call-update) | async-done | bytes 4194320 | tf_op jit(solution)/shard_map/all_gather | solution.py:29
  217.4 4.1 multiply_convert_fusion.1
  221.5 0.0 copy-done.1
  221.5 0.0 copy-start.2
  221.5 1.3 fusion.8
  222.8 0.3 copy-done.2
  223.1 4.5 convolution_add_fusion
  227.6 0.0 reduce-scatter.3.cloned.1.call-update
  227.6 0.0 reduce-scatter.5.cloned.1.call-start
  227.6 0.0 copy-start
  227.6 3.1 fusion.1
  230.8 0.3 copy-done
  231.1 0.0 copy-start.3
  231.1 0.8 fusion.2
  231.9 2.1 copy-done.3
  234.0 0.8 fusion
  234.8 5.0 %pad_maximum_fusion = f32[8192,384]{0,1:T(8,128)} fusion(f32[8192,128]{0,1:T(8,128)S(1)} %fusion, f32[8192,128]{0,1:T(8,128)S(1)} %fusion.1, f32[8192,128]{0,1:T(8,128)S(1)} %fusion.2), kind=kLoop, calls=%fused_computation | loop fusion | flops 6291456 | bytes 25165824 | tf_op jit(solution)/shard_map/concatenate | solution.py:59
  239.8 0.0 reduce-scatter.5.cloned.1.call-update
  239.9 76.2 %reduce-scatter.3.cloned.1.call-done = f32[256,1024]{1,0:T(8,128)} async-done(((f32[256,8192]{1,0:T(8,128)}), f32[256,1024]{1,0:T(8,128)}) %reduce-scatter.3.cloned.1.call-update) | async-done | bytes 1048592 | tf_op jit(solution)/shard_map/reduce_scatter | solution.py:53
  316.1 2.1 convert_element_type.14
  318.2 120.1 %reduce-scatter.5.cloned.1.call-done = f32[2048,384]{0,1:T(8,128)} async-done(((f32[8192,384]{0,1:T(8,128)}), f32[2048,384]{0,1:T(8,128)}) %reduce-scatter.5.cloned.1.call-update) | async-done | bytes 3145744 | tf_op jit(solution)/shard_map/reduce_scatter | solution.py:15
  438.3 3.1 slice_bitcast_fusion
  441.4 1.3 copy.9
  442.7 1.3 copy.10
Async XLA Ops:
  7.2 40.6 %all-gather.14.cloned.1.call-start = ((), (), s32[]{:S(2)}) async-start(), calls=%async_computation.6 | async-start | bytes 2621440 | tf_op jit(solution)/shard_map/all_gather | solution.py:31
  7.9 88.4 %all-gather.10.cloned.1.call-start = ((), (), s32[]{:S(2)}) async-start(), calls=%async_computation.4 | async-start | bytes 4718592 | tf_op jit(solution)/shard_map/all_gather | solution.py:28
  8.6 123.5 %all-gather.12.cloned.1.call-start = ((), (), s32[]{:S(2)}) async-start(), calls=%async_computation.5 | async-start | bytes 2621440 | tf_op jit(solution)/shard_map/all_gather | solution.py:32
  9.4 159.6 %all-gather.8.cloned.1.call-start = ((), (), s32[]{:S(2)}) async-start(), calls=%async_computation.3 | async-start | bytes 2621440 | tf_op jit(solution)/shard_map/all_gather | solution.py:9
  10.0 207.4 %all-gather.6.cloned.1.call-start = ((), (), s32[]{:S(2)}) async-start(), calls=%async_computation.2 | async-start | bytes 4718592 | tf_op jit(solution)/shard_map/all_gather | solution.py:29
  10.5 305.5 %reduce-scatter.3.cloned.1.call-start = ((), (), s32[]{:S(2)}) async-start(), calls=%async_computation.7 | async-start | bytes 9437184 | tf_op jit(solution)/shard_map/reduce_scatter | solution.py:53
  136.2 85.3 %copy-start.1 = (bf16[8192,128]{1,0:T(8,128)(2,1)S(1)}, bf16[8192,128]{1,0:T(8,128)(2,1)}, u32[]{:S(2)}) copy-start(bf16[8192,128]{1,0:T(8,128)(2,1)} %all-gather.14.cloned.1.call-done) | copy-start | bytes 6291460
  221.5 1.6 copy-start.2
  227.6 210.7 %reduce-scatter.5.cloned.1.call-start = ((), (), s32[]{:S(2)}) async-start(), calls=%async_computation.8 | async-start | bytes 15728640 | tf_op jit(solution)/shard_map/reduce_scatter | solution.py:15
  227.6 3.5 copy-start
  231.1 2.9 copy-start.3
Sparse Core Ops, SparseCore 0:
  9.8 37.8 all-gather.13
  49.4 46.8 all-gather.9
  98.1 33.9 all-gather.11
  133.8 35.1 all-gather.7
  170.5 46.8 all-gather.5
  227.7 88.3 reduce-scatter.2
  319.2 119.0 reduce-scatter.4
where the time goes:
time: 451 us
  waiting for transfers between devices  398 us (88%)
  matrix products  22.8 us (5%)
  between operations  14.2 us (3%)
  local copies, waits for them, and re-layouts  8.46 us (2%)
  other arithmetic  7.1 us (2%)
    reduce_scatter x1, waiting for transfers between devices, own_rows(): lax.psum_scatter(portion(jnp.int32(0), count), axis, scatter_dimension=0,...  120 us
    reduce_scatter x1, waiting for transfers between devices, body(): lax.psum_scatter(partial_term, 'tp', scatter_dimension=1, tiled=True)  76.2 us
    all_gather x1, waiting for transfers between devices, body(): whole = lax.all_gather(tokens, 'tp', axis=1, tiled=True)  48.5 us
    all_gather x1, waiting for transfers between devices, body(): grads = lax.all_gather(out_grad, 'tp', axis=1, tiled=True)  48.4 us
    all_gather x1, waiting for transfers between devices, body(): lax.all_gather(gate_weight, 'fsdp', axis=0, tiled=True)  37.2 us
    all_gather x1, waiting for transfers between devices, over_all(): lax.all_gather(a, axis, axis=dim, tiled=True)  32.8 us
    all_gather x1, waiting for transfers between devices, body(): lax.all_gather(up_weight, 'fsdp', axis=0, tiled=True)  31.8 us
  transfers between devices with their start and end apart: 7, of which 7 were waited for; matrix products, arithmetic and copies ran while one was open for 4% of the time, Pallas kernels for 0%

commit v1 on v0

--- a/solution.py
+++ b/solution.py
@@ -25,8 +25,11 @@
 
 def body(tokens, out_grad, gate_weight, up_weight, down_weight):
     factor = 1.0 / math.sqrt(tokens.shape[0] * lax.axis_size("fsdp"))
-    whole = lax.all_gather(tokens, "tp", axis=1, tiled=True)
-    grads = lax.all_gather(out_grad, "tp", axis=1, tiled=True)
+    whole, grads = jnp.split(
+        lax.all_gather(jnp.concatenate([tokens, out_grad], axis=0), "tp", axis=1, tiled=True),
+        [tokens.shape[0]],
+        axis=0,
+    )
     gate_full, up_full = (
         lax.all_gather(gate_weight, "fsdp", axis=0, tiled=True),
         lax.all_gather(up_weight, "fsdp", axis=0, tiled=True),

time: 451 us -> 439 us (0.973)
  waiting for transfers between devices: 398 us -> 383 us
    all_gather x2 -> x1, waiting for transfers between devices: 96.9 us -> 84.2 us  [body(): lax.all_gather(jnp.concatenate([tokens, out_grad], axis=0), 'tp', axis=1,...]
  transfers between devices with their start and end apart: 7 -> 6, of which waited for: 7 -> 6; matrix products, arithmetic and copies ran while one was open for 4% -> 6% of each run, Pallas kernels for 0% -> 0%
where the time goes in v1:
time: 439 us
  waiting for transfers between devices  383 us (87%)
  matrix products  25.2 us (6%)
  between operations  14.2 us (3%)
  other arithmetic  9.29 us (2%)
  local copies, waits for them, and re-layouts  6.94 us (2%)
    reduce_scatter x1, waiting for transfers between devices, own_rows(): lax.psum_scatter(portion(jnp.int32(0), count), axis, scatter_dimension=0,...  120 us
    all_gather x1, waiting for transfers between devices, body(): lax.all_gather(jnp.concatenate([tokens, out_grad], axis=0), 'tp', axis=1,...  84.2 us
    reduce_scatter x1, waiting for transfers between devices, body(): lax.psum_scatter(partial_term, 'tp', scatter_dimension=1, tiled=True)  76.5 us
    all_gather x1, waiting for transfers between devices, body(): lax.all_gather(gate_weight, 'fsdp', axis=0, tiled=True)  36.2 us
    all_gather x1, waiting for transfers between devices, over_all(): lax.all_gather(a, axis, axis=dim, tiled=True)  32.8 us
    all_gather x1, waiting for transfers between devices, body(): lax.all_gather(up_weight, 'fsdp', axis=0, tiled=True)  31.4 us
  transfers between devices with their start and end apart: 6, of which 6 were waited for; matrix products, arithmetic and copies ran while one was open for 6% of the time, Pallas kernels for 0%

profile of v1, /device:TPU:0, one launch (start us, length us, event | category | flops | bytes accessed | tf_op | source)
XLA Modules:
  0.0 439.0 jit_solution(5686850107040670691)
XLA Ops:
  7.2 0.0 all-gather.11.cloned.1.call-start
  7.2 0.7 all-gather.11.cloned.1.call-update
  7.9 0.0 all-gather.5.cloned.1.call-start
  7.9 2.2 pad_maximum_fusion.1
  10.2 0.0 all-gather.5.cloned.1.call-update
  10.2 0.0 all-gather.9.cloned.1.call-start
  10.3 0.7 all-gather.9.cloned.1.call-update
  10.9 0.0 all-gather.7.cloned.1.call-start
  11.0 0.5 all-gather.7.cloned.1.call-update
  11.5 0.0 reduce-scatter.3.cloned.1.call-start
  11.6 36.2 %all-gather.11.cloned.1.call-done = bf16[8192,128]{1,0:T(8,128)(2,1)} async-done(((bf16[2048,128]{1,0:T(8,128)(2,1)}), bf16[8192,128]{1,0:T(8,128)(2,1)}) %all-gather.11.cloned.1.call-update) | async-done | bytes 2097168 | tf_op jit(solution)/shard_map/all_gather | solution.py:34
  47.8 84.2 %all-gather.5.cloned.1.call-done = bf16[512,8192]{1,0:T(8,128)(2,1)} async-done(((bf16[512,1024]{1,0:T(8,128)(2,1)}), bf16[512,8192]{1,0:T(8,128)(2,1)}) %all-gather.5.cloned.1.call-update) | async-done | bytes 8388624 | tf_op jit(solution)/shard_map/all_gather | solution.py:29
  132.0 4.1 fusion.5
  136.1 31.4 %all-gather.9.cloned.1.call-done = bf16[8192,128]{1,0:T(8,128)(2,1)} async-done(((bf16[2048,128]{1,0:T(8,128)(2,1)}), bf16[8192,128]{1,0:T(8,128)(2,1)}) %all-gather.9.cloned.1.call-update) | async-done | bytes 2097168 | tf_op jit(solution)/shard_map/all_gather | solution.py:35
  167.5 4.1 fusion.7
  171.7 0.0 copy-start
  171.7 32.8 %all-gather.7.cloned.1.call-done = bf16[128,8192]{1,0:T(8,128)(2,1)} async-done(((bf16[128,2048]{1,0:T(8,128)(2,1)}), bf16[128,8192]{1,0:T(8,128)(2,1)}) %all-gather.7.cloned.1.call-update) | async-done | bytes 2097168 | tf_op jit(solution)/shard_map/all_gather | solution.py:9
  204.5 4.1 multiply_convert_fusion.1
  208.6 0.0 copy-done
  208.6 0.0 copy-start.1
  208.6 1.3 fusion.12
  209.9 0.3 copy-done.1
  210.2 4.5 %convolution_add_fusion = f32[256,8192]{1,0:T(8,128)} fusion(f32[256,8192]{1,0:T(8,128)S(1)} %fusion.12, bf16[256,128]{1,0:T(8,128)(2,1)S(1)} %get-tuple-element.11, bf16[8192,128]{1,0:T(8,128)(2,1)S(1)} %copy-done.1), kind=kOutput, calls=%fused_computation.1 | convolution fusion | flops 538968064 | bytes 18939904 | tf_op jit(solution)/shard_map/dot_general | solution.py:55
  214.6 0.0 reduce-scatter.3.cloned.1.call-update
  214.7 0.0 reduce-scatter.5.cloned.1.call-start
  214.7 0.0 slice-start
  214.7 3.2 convolution_multiply_fusion.1
  217.9 0.0 slice-start.1
  217.9 3.2 convolution_multiply_fusion.2
  221.1 0.0 slice-done
  221.1 0.9 slice-done.1
  222.0 0.8 convolution_multiply_fusion
  222.8 5.0 %pad_maximum_fusion = f32[8192,384]{0,1:T(8,128)} fusion(f32[8192,128]{0,1:T(8,128)S(1)} %convolution_multiply_fusion, f32[8192,128]{0,1:T(8,128)S(1)} %convolution_multiply_fusion.1, f32[8192,128]{0,1:T(8,128)S(1)} %convolution_multiply_fusion.2), kind=kLoop, calls=%fused_computation | loop fusion | flops 6291456 | bytes 25165824 | tf_op jit(solution)/shard_map/concatenate | solution.py:62
  227.8 0.0 reduce-scatter.5.cloned.1.call-update
  227.8 76.5 %reduce-scatter.3.cloned.1.call-done = f32[256,1024]{1,0:T(8,128)} async-done(((f32[256,8192]{1,0:T(8,128)}), f32[256,1024]{1,0:T(8,128)}) %reduce-scatter.3.cloned.1.call-update) | async-done | bytes 1048592 | tf_op jit(solution)/shard_map/reduce_scatter | solution.py:56
  304.3 2.1 convert_element_type.14
  306.4 120.0 %reduce-scatter.5.cloned.1.call-done = f32[2048,384]{0,1:T(8,128)} async-done(((f32[8192,384]{0,1:T(8,128)}), f32[2048,384]{0,1:T(8,128)}) %reduce-scatter.5.cloned.1.call-update) | async-done | bytes 3145744 | tf_op jit(solution)/shard_map/reduce_scatter | solution.py:15
  426.4 3.1 slice_bitcast_fusion
  429.5 1.3 copy.9
  430.8 1.3 copy.10
  (1 shorter events, 0.0 us)
Async XLA Ops:
  7.2 40.6 %all-gather.11.cloned.1.call-start = ((), (), s32[]{:S(2)}) async-start(), calls=%async_computation.5 | async-start | bytes 2621440 | tf_op jit(solution)/shard_map/all_gather | solution.py:34
  7.9 124.1 %all-gather.5.cloned.1.call-start = ((), (), s32[]{:S(2)}) async-start(), calls=%async_computation.2 | async-start | bytes 9437184 | tf_op jit(solution)/shard_map/all_gather | solution.py:29
  10.2 157.3 %all-gather.9.cloned.1.call-start = ((), (), s32[]{:S(2)}) async-start(), calls=%async_computation.4 | async-start | bytes 2621440 | tf_op jit(solution)/shard_map/all_gather | solution.py:35
  10.9 193.5 %all-gather.7.cloned.1.call-start = ((), (), s32[]{:S(2)}) async-start(), calls=%async_computation.3 | async-start | bytes 2621440 | tf_op jit(solution)/shard_map/all_gather | solution.py:9
  11.5 292.8 %reduce-scatter.3.cloned.1.call-start = ((), (), s32[]{:S(2)}) async-start(), calls=%async_computation.6 | async-start | bytes 9437184 | tf_op jit(solution)/shard_map/reduce_scatter | solution.py:56
  171.7 36.9 %copy-start = (bf16[8192,128]{1,0:T(8,128)(2,1)S(1)}, bf16[8192,128]{1,0:T(8,128)(2,1)}, u32[]{:S(2)}) copy-start(bf16[8192,128]{1,0:T(8,128)(2,1)} %all-gather.11.cloned.1.call-done) | copy-start | bytes 6291460
  208.6 1.6 copy-start.1
  214.7 211.8 %reduce-scatter.5.cloned.1.call-start = ((), (), s32[]{:S(2)}) async-start(), calls=%async_computation.7 | async-start | bytes 15728640 | tf_op jit(solution)/shard_map/reduce_scatter | solution.py:15
  214.7 6.3 %slice-start = ((s8[8388608]{0:T(1024)(128)(4,1)}), s8[4194304]{0:T(1024)(128)(4,1)S(1)}, s32[]{:S(2)}) async-start(s8[8388608]{0:T(1024)(128)(4,1)} %bitcast.11), calls=%async_computation.8 | async-start | bytes 8388608
  217.9 4.1 slice-start.1
Sparse Core Ops, SparseCore 0:
  9.8 37.8 all-gather.10
  49.9 82.0 all-gather.4
  133.8 33.6 all-gather.8
  169.2 35.1 all-gather.6
  214.8 89.4 reduce-scatter.2
  307.3 119.0 reduce-scatter.4
